TPU v7x, 32 devices: a whole 2x2x4 slice. The times are simulated.
32 devices in a mesh: dp: 8 (over z, x), seq: 4 (over y, core).
Axes of the slice: x: 2, y: 2, z: 4, core: 2. Of those that a mesh axis runs over, the one named last changes fastest.
Arguments:
- short_input: bfloat16 [192, 128, 1024], P(('dp', 'seq')), may hold values from -6 to 6
- long_input: bfloat16 [16, 512, 1024], P('dp', 'seq'), may hold values from -6 to 6
- short_cotangent: bfloat16 [192, 128, 1024], P(('dp', 'seq')), may hold values from -6 to 6
- long_cotangent: bfloat16 [16, 512, 1024], P('dp', 'seq'), may hold values from -6 to 6
- short_lengths: int32 [192], P(('dp', 'seq')), may hold values from 32 to 128, as said below
- long_lengths: int32 [16], P('dp'), may hold values from 128 to 512, as said below
- query_weight: float32 [1024, 1024], P(('dp', 'seq')), may hold values from -0.1875 to 0.1875
- key_weight: float32 [1024, 1024], P(('dp', 'seq')), may hold values from -0.1875 to 0.1875
- value_weight: float32 [1024, 1024], P(('dp', 'seq')), may hold values from -0.1875 to 0.1875
- output_weight: float32 [1024, 1024], P(('dp', 'seq')), may hold values from -0.75 to 0.75
- upward_weight: float32 [1024, 4096], P(('dp', 'seq')), may hold values from -0.1875 to 0.1875
- downward_weight: float32 [4096, 1024], P(('dp', 'seq')), may hold values from -0.09375 to 0.09375
- query_bias: float32 [1024], replicated, may hold values from -3 to 3
- value_bias: float32 [1024], replicated, may hold values from -3 to 3
- output_bias: float32 [1024], replicated, may hold values from -3 to 3
- upward_bias: float32 [4096], replicated, may hold values from -3 to 3
- downward_bias: float32 [1024], replicated, may hold values from -3 to 3
- first_gain: float32 [1024], replicated, may hold values from 0.25 to 1.75
- first_shift: float32 [1024], replicated, may hold values from -3 to 3
- second_gain: float32 [1024], replicated, may hold values from 0.25 to 1.75
- second_shift: float32 [1024], replicated, may hold values from -3 to 3
Outputs:
- short_output: bfloat16 [192, 128, 1024], P(('dp', 'seq'))
- long_output: bfloat16 [16, 512, 1024], P('dp', 'seq')
- short_grad: bfloat16 [192, 128, 1024], P(('dp', 'seq'))
- long_grad: bfloat16 [16, 512, 1024], P('dp', 'seq')
- query_delta: float32 [1024], replicated
- value_delta: float32 [1024], replicated
- output_delta: float32 [1024], replicated
- upward_delta: float32 [4096], replicated
- downward_delta: float32 [1024], replicated
- first_delta: float32 [1024], replicated
- second_delta: float32 [1024], replicated
Inputs may be any that keep to these rules, and one draw needn't show every extreme that they name: `short_lengths`: some short sequence has all 128 positions. `long_lengths`: some long sequence has all 512 positions.
All inputs are finite; a program needn't handle non-finite values.
Results may differ from a plain program's by a relative error of at most 0.013.
The roundings to bfloat16 on the way count: a program that leaves them out, or rounds other values in their place, can miss the bound.
Values may be sent and summed in bfloat16 or wider, within the bound.
A program may use at most 192 MiB of HBM per device.

v0:
```python
import jax
import jax.numpy as jnp
from jax import lax
from jax.sharding import PartitionSpec as P

HEADS = 16
HEAD = 64
epsilon = 1e-12
masked = -1e30


def forward_product(left, right):
    return jnp.dot(left, right, preferred_element_type=jnp.float32)


def backward_product(left, right):
    return lax.dot_general(
        left, right, (((left.ndim - 1,), (1,)), ((), ())), preferred_element_type=jnp.float32
    )


def exact_backward(left, right):
    return lax.dot_general(
        left,
        right,
        (((left.ndim - 1,), (1,)), ((), ())),
        precision=lax.Precision.HIGHEST,
        preferred_element_type=jnp.float32,
    )


def norm_apply(value, gain, shift):
    center = value - jnp.mean(value, axis=-1, keepdims=True)
    spread = jnp.mean(center * center, axis=-1, keepdims=True)
    return center * lax.rsqrt(spread + epsilon) * gain + shift


def token_total(value):
    return jnp.sum(value, axis=(0, 1))


def keep_local(first_part, second_part):
    return (first_part, second_part)


def spread_long(key_rows, values):
    return (
        lax.all_gather(key_rows, "seq", axis=1, tiled=True),
        lax.all_gather(values, "seq", axis=1, tiled=True),
    )


def settle_each(value):
    return lax.psum(value, ("dp", "seq"))


def finish_local(key_terms, value_terms, key_exact, value_exact, settle):
    value_delta = settle(token_total(value_terms))
    through = exact_backward(key_terms, key_exact) + exact_backward(value_terms, value_exact)
    return (through, value_delta)


def finish_summed(key_terms, value_terms, key_exact, value_exact, settle):
    key_grad, value_grad = (
        lax.psum_scatter(
            key_terms.astype(jnp.bfloat16), "seq", scatter_dimension=1, tiled=True
        ).astype(jnp.float32),
        lax.psum_scatter(
            value_terms.astype(jnp.bfloat16), "seq", scatter_dimension=1, tiled=True
        ).astype(jnp.float32),
    )
    value_delta = settle(token_total(value_grad))
    through = exact_backward(key_grad, key_exact) + exact_backward(value_grad, value_exact)
    return (through, value_delta)


def recompute(inputs, usable, weights, params, spread):
    query_weight, key_weight, value_weight, output_weight, upward_weight, downward_weight = weights
    (
        query_bias,
        value_bias,
        output_bias,
        upward_bias,
        downward_bias,
        first_gain,
        first_shift,
        second_gain,
        second_shift,
    ) = params
    number, seqlen, breadth = inputs.shape
    queries = (forward_product(inputs, query_weight) + query_bias).astype(jnp.bfloat16)
    key_rows = forward_product(inputs, key_weight).astype(jnp.bfloat16)
    values = (forward_product(inputs, value_weight) + value_bias).astype(jnp.bfloat16)
    key_all, value_all = spread(key_rows, values)
    query_heads = queries.reshape(number, seqlen, HEADS, HEAD)
    key_heads = key_all.reshape(number, key_all.shape[1], HEADS, HEAD)
    value_heads = value_all.reshape(number, value_all.shape[1], HEADS, HEAD)
    scores = jnp.einsum(
        "nqhd,nkhd->nhqk", query_heads, key_heads, preferred_element_type=jnp.float32
    ) * HEAD ** (-0.5)
    scores = jnp.where(usable[:, None, None, :], scores, masked)
    attention = jax.nn.softmax(scores, axis=-1)
    attention_low = attention.astype(jnp.bfloat16)
    blended = jnp.einsum(
        "nhqk,nkhd->nqhd", attention_low, value_heads, preferred_element_type=jnp.float32
    )
    blended = blended.reshape(number, seqlen, breadth).astype(jnp.bfloat16)
    residual = inputs.astype(jnp.float32) + forward_product(blended, output_weight) + output_bias
    normed = norm_apply(residual, first_gain, first_shift)
    pre_up = forward_product(normed.astype(jnp.bfloat16), upward_weight) + upward_bias
    active = jax.nn.gelu(pre_up, approximate=True).astype(jnp.bfloat16)
    ffn_sum = normed + forward_product(active, downward_weight) + downward_bias
    output = norm_apply(ffn_sum, second_gain, second_shift)
    return (
        query_heads,
        key_heads,
        value_heads,
        attention,
        attention_low,
        residual,
        pre_up,
        ffn_sum,
        output,
    )


def backprop(inputs, cotangent, usable, weights, params, spread, finish, settle):
    (
        query_heads,
        key_heads,
        value_heads,
        attention,
        attention_low,
        residual,
        pre_up,
        ffn_sum,
        output,
    ) = recompute(inputs, usable, weights, params, spread)
    query_weight, key_weight, value_weight, output_weight, upward_weight, downward_weight = weights
    (
        query_bias,
        value_bias,
        output_bias,
        upward_bias,
        downward_bias,
        first_gain,
        first_shift,
        second_gain,
        second_shift,
    ) = params
    number, seqlen, breadth = inputs.shape
    upstream = cotangent.astype(jnp.float32)
    second_pull = jax.vjp(lambda value: norm_apply(value, second_gain, second_shift), ffn_sum)[1]
    ffn_grad = second_pull(upstream)[0]
    second_delta = settle(token_total(upstream))
    downward_delta = settle(token_total(ffn_grad))
    active_grad = backward_product(ffn_grad.astype(jnp.bfloat16), downward_weight)
    gelu_pull = jax.vjp(lambda value: jax.nn.gelu(value, approximate=True), pre_up)[1]
    pre_grad = gelu_pull(active_grad)[0]
    upward_delta = settle(token_total(pre_grad))
    normed_grad = ffn_grad + backward_product(pre_grad.astype(jnp.bfloat16), upward_weight)
    first_delta = settle(token_total(normed_grad))
    first_pull = jax.vjp(lambda value: norm_apply(value, first_gain, first_shift), residual)[1]
    residual_grad = first_pull(normed_grad)[0]
    output_delta = settle(token_total(residual_grad))
    blended_grad = backward_product(residual_grad.astype(jnp.bfloat16), output_weight).astype(
        jnp.bfloat16
    )
    blended_grad = blended_grad.reshape(number, seqlen, HEADS, HEAD)
    prob_grad = jnp.einsum(
        "nqhd,nkhd->nhqk", blended_grad, value_heads, preferred_element_type=jnp.float32
    )
    score_grad = attention * (prob_grad - jnp.sum(prob_grad * attention, axis=-1, keepdims=True))
    score_grad = score_grad.astype(jnp.bfloat16)
    query_grad = jnp.einsum(
        "nhqk,nkhd->nqhd", score_grad, key_heads, preferred_element_type=jnp.float32
    )
    query_grad = query_grad.reshape(number, seqlen, breadth) * HEAD ** (-0.5)
    key_terms = jnp.einsum(
        "nhqk,nqhd->nkhd", score_grad, query_heads, preferred_element_type=jnp.float32
    )
    key_terms = key_terms.reshape(number, key_heads.shape[1], breadth) * HEAD ** (-0.5)
    value_terms = jnp.einsum(
        "nhqk,nqhd->nkhd", attention_low, blended_grad, preferred_element_type=jnp.float32
    )
    value_terms = value_terms.reshape(number, value_heads.shape[1], breadth)
    key_exact = key_weight.astype(jnp.float32)
    value_exact = value_weight.astype(jnp.float32)
    through, value_delta = finish(key_terms, value_terms, key_exact, value_exact, settle)
    query_delta = settle(token_total(query_grad))
    input_grad = (
        residual_grad + backward_product(query_grad.astype(jnp.bfloat16), query_weight) + through
    )
    deltas = (
        query_delta,
        value_delta,
        output_delta,
        upward_delta,
        downward_delta,
        first_delta,
        second_delta,
    )
    return (input_grad.astype(jnp.bfloat16), deltas)


def on_device(
    short_input,
    long_input,
    short_cotangent,
    long_cotangent,
    short_lengths,
    long_lengths,
    query_weight,
    key_weight,
    value_weight,
    output_weight,
    upward_weight,
    downward_weight,
    query_bias,
    value_bias,
    output_bias,
    upward_bias,
    downward_bias,
    first_gain,
    first_shift,
    second_gain,
    second_shift,
):
    params = (
        query_bias,
        value_bias,
        output_bias,
        upward_bias,
        downward_bias,
        first_gain,
        first_shift,
        second_gain,
        second_shift,
    )
    short_usable = jnp.arange(short_input.shape[1])[None, :] < short_lengths[:, None]
    long_span = long_input.shape[1] * lax.axis_size("seq")
    long_usable = jnp.arange(long_span)[None, :] < long_lengths[:, None]
    query_low = query_weight.astype(jnp.bfloat16)
    key_low = key_weight.astype(jnp.bfloat16)
    value_low = value_weight.astype(jnp.bfloat16)
    output_low = output_weight.astype(jnp.bfloat16)
    upward_low = upward_weight.astype(jnp.bfloat16)
    downward_low = downward_weight.astype(jnp.bfloat16)
    gathered = (
        lax.all_gather(query_low, ("dp", "seq"), axis=0, tiled=True),
        lax.all_gather(key_low, ("dp", "seq"), axis=0, tiled=True),
        lax.all_gather(value_low, ("dp", "seq"), axis=0, tiled=True),
        lax.all_gather(output_low, ("dp", "seq"), axis=0, tiled=True),
        lax.all_gather(upward_low, ("dp", "seq"), axis=0, tiled=True),
        lax.all_gather(downward_low, ("dp", "seq"), axis=0, tiled=True),
    )
    short_output = recompute(short_input, short_usable, gathered, params, keep_local)[-1]
    long_output = recompute(long_input, long_usable, gathered, params, spread_long)[-1]
    regathered = (
        lax.all_gather(query_low, ("dp", "seq"), axis=0, tiled=True),
        lax.all_gather(key_low, ("dp", "seq"), axis=0, tiled=True),
        lax.all_gather(value_low, ("dp", "seq"), axis=0, tiled=True),
        lax.all_gather(output_low, ("dp", "seq"), axis=0, tiled=True),
        lax.all_gather(upward_low, ("dp", "seq"), axis=0, tiled=True),
        lax.all_gather(downward_low, ("dp", "seq"), axis=0, tiled=True),
    )
    short_grad, short_deltas = backprop(
        short_input,
        short_cotangent,
        short_usable,
        regathered,
        params,
        keep_local,
        finish_local,
        settle_each,
    )
    long_grad, long_deltas = backprop(
        long_input,
        long_cotangent,
        long_usable,
        regathered,
        params,
        spread_long,
        finish_summed,
        settle_each,
    )
    summed = tuple(
        (first_part + second_part for first_part, second_part in zip(short_deltas, long_deltas))
    )
    return (
        short_output.astype(jnp.bfloat16),
        long_output.astype(jnp.bfloat16),
        short_grad,
        long_grad,
        summed[0],
        summed[1],
        summed[2],
        summed[3],
        summed[4],
        summed[5],
        summed[6],
    )


def solution(mesh):
    placed = (
        P(("dp", "seq"), None, None),
        P("dp", "seq", None),
        P(("dp", "seq"), None, None),
        P("dp", "seq", None),
        P(("dp", "seq")),
        P("dp"),
        P(("dp", "seq"), None),
        P(("dp", "seq"), None),
        P(("dp", "seq"), None),
        P(("dp", "seq"), None),
        P(("dp", "seq"), None),
        P(("dp", "seq"), None),
        P(),
        P(),
        P(),
        P(),
        P(),
        P(),
        P(),
        P(),
        P(),
    )
    return jax.shard_map(
        on_device,
        mesh=mesh,
        in_specs=placed,
        out_specs=(
            P(("dp", "seq"), None, None),
            P("dp", "seq", None),
            P(("dp", "seq"), None, None),
            P("dp", "seq", None),
            P(),
            P(),
            P(),
            P(),
            P(),
            P(),
            P(),
        ),
        check_vma=False,
    )
```

profile of v0, /device:TPU:0, one launch (start us, length us, event | category | flops | bytes accessed | tf_op | source)
XLA Modules:
  0.0 694.6 jit_solution(11124600776407439953)
XLA Ops:
  13.7 56.7 %all-gather.9.cloned.1.call-done = bf16[1024,1024]{1,0:T(8,128)(2,1)} async-done(((bf16[32,1024]{1,0:T(8,128)(2,1)}), bf16[1024,1024]{1,0:T(8,128)(2,1)}) %all-gather.9.cloned.1.call-update) | async-done | bytes 2097168 | tf_op jit(solution)/shard_map/all_gather | solution.py:252
  73.7 55.3 %all-gather.13.cloned.1.call-done = bf16[1024,1024]{1,0:T(8,128)(2,1)} async-done(((bf16[32,1024]{1,0:T(8,128)(2,1)}), bf16[1024,1024]{1,0:T(8,128)(2,1)}) %all-gather.13.cloned.1.call-update) | async-done | bytes 2097168 | tf_op jit(solution)/shard_map/all_gather | solution.py:251
  134.0 53.6 %all-gather.11.cloned.1.call-done = bf16[1024,1024]{1,0:T(8,128)(2,1)} async-done(((bf16[32,1024]{1,0:T(8,128)(2,1)}), bf16[1024,1024]{1,0:T(8,128)(2,1)}) %all-gather.11.cloned.1.call-update) | async-done | bytes 2097168 | tf_op jit(solution)/shard_map/all_gather | solution.py:250
  219.2 26.2 %all-gather.15.cloned.1.call-done = bf16[1024,1024]{1,0:T(8,128)(2,1)} async-done(((bf16[32,1024]{1,0:T(8,128)(2,1)}), bf16[1024,1024]{1,0:T(8,128)(2,1)}) %all-gather.15.cloned.1.call-update) | async-done | bytes 2097168 | tf_op jit(solution)/shard_map/all_gather | solution.py:253
  251.0 17.8 %all-gather.21.cloned.1.call-done = bf16[2,512,1024]{2,1,0:T(8,128)(2,1)} async-done(((bf16[2,128,1024]{2,1,0:T(8,128)(2,1)}), bf16[2,512,1024]{2,1,0:T(8,128)(2,1)}) %all-gather.21.cloned.1.call-update) | async-done | bytes 2097168 | tf_op jit(solution)/shard_map/all_gather | solution.py:49
  272.8 20.0 %all-gather.23.cloned.1.call-done = bf16[2,512,1024]{2,1,0:T(8,128)(2,1)} async-done(((bf16[2,128,1024]{2,1,0:T(8,128)(2,1)}), bf16[2,512,1024]{2,1,0:T(8,128)(2,1)}) %all-gather.23.cloned.1.call-update) | async-done | bytes 2097168 | tf_op jit(solution)/shard_map/all_gather | solution.py:48
  297.1 7.9 %fusion.219 = (f32[2,16,128]{2,1,0:T(8,128)S(1)}, f32[2,16,128,512]{3,2,1,0:T(8,128)}) fusion(pred[2,512]{1,0:T(4,128)(4,1)S(1)} %iota_compare_fusion, bf16[2,128,16,64]{1,3,2,0:T(8,128)(2,1)} %bitcast.210, bf16[2,512,16,64]{1,3,2,0:T(8,128)(2,1)} %bitcast.198), kind=kOutput, calls=%fused_computation.229 | convolution fusion | flops 276824576 | bytes 11027456 | tf_op jit(solution)/shard_map/sub | solution.py:102
  312.9 59.9 %all-gather.17.cloned.1.call-done = bf16[1024,4096]{1,0:T(8,128)(2,1)} async-done(((bf16[32,4096]{1,0:T(8,128)(2,1)}), bf16[1024,4096]{1,0:T(8,128)(2,1)}) %all-gather.17.cloned.1.call-update) | async-done | bytes 8388624 | tf_op jit(solution)/shard_map/all_gather | solution.py:254
  372.8 8.1 %fusion.30 = f32[2,128,4096]{2,1,0:T(8,128)} fusion(bf16[1024,4096]{1,0:T(8,128)(2,1)} %all-gather.17.cloned.1.call-done, f32[4096]{0:T(1024)S(1)} %copy-done.49, f32[2,128,1024]{2,1,0:T(8,128)} %copy-done.11, f32[1024]{0:T(1024)S(1)} %copy-done.53, f32[1024]{0:T(1024)S(1)} %copy-done.46, f32[2,128]{1,0:T(2,128)S(1)} %fusion.195, ...), kind=kOutput, calls=%fused_computation.43 | convolution fusion | flops 2149842944 | bytes 13658112 | tf_op jit(solution)/shard_map/dot_general | solution.py:13
  380.9 70.5 %all-gather.19.cloned.1.call-done = bf16[4096,1024]{1,0:T(8,128)(2,1)} async-done(((bf16[128,1024]{1,0:T(8,128)(2,1)}), bf16[4096,1024]{1,0:T(8,128)(2,1)}) %all-gather.19.cloned.1.call-update) | async-done | bytes 8388624 | tf_op jit(solution)/shard_map/all_gather | solution.py:255
  451.4 7.8 %fusion.221 = (f32[2,128]{1,0:T(2,128)S(1)}, f32[2,128,1024]{2,1,0:T(8,128)S(1)}) fusion(f32[1024]{0:T(1024)S(1)} %copy-done.52, bf16[4096,1024]{1,0:T(8,128)(2,1)} %all-gather.19.cloned.1.call-done, f32[2,128,4096]{2,1,0:T(8,128)} %fusion.30, f32[1024]{0:T(1024)S(1)} %copy-done.53, f32[1024]{0:T(1024)S(1)} %copy-done.46, f32[2,128]{1,0:T(2,128)S(1)} %fusion.195, ...), kind=kOutput, calls=%fused_computation.231 | convolution fusion | flops 2158755584 | bytes 14695424 | tf_op jit(solution)/shard_map/dot_general | solution.py:13
  460.1 8.3 %fusion.223 = (f32[4096]{0:T(1024)S(1)}, bf16[2,128,4096]{2,1,0:T(8,128)(2,1)S(1)}) fusion(f32[2,128,4096]{2,1,0:T(8,128)S(1)} %copy-done.56, bf16[4096,1024]{1,0:T(8,128)(2,1)} %all-gather.19.cloned.1.call-done, f32[2,128]{1,0:T(2,128)S(1)} %negate_multiply_fusion.3, f32[2,128]{1,0:T(2,128)S(1)} %get-tuple-element.42, ...), kind=kOutput, calls=%fused_computation.233 | convolution fusion | flops 2171858944 | bytes 16277504 | tf_op jit(solution)/shard_map/dot_general | solution.py:17
  476.9 5.9 fusion.95
  482.8 6.5 multiply_reduce_fusion
  493.3 13.0 %fusion.22 = f32[6,128,4096]{2,1,0:T(8,128)} fusion(bf16[1024,4096]{1,0:T(8,128)(2,1)} %all-gather.17.cloned.1.call-done, f32[6,128,1024]{2,1,0:T(8,128)S(1)} %get-tuple-element.47, f32[1024]{0:T(1024)S(1)} %copy-done.53, f32[1024]{0:T(1024)S(1)} %copy-done.46, f32[6,128]{1,0:T(8,128)S(1)} %fusion.193, f32[6,128]{1,0:T(8,128)S(1)} %broadcast_multiply_fusion.1), kind=kOutput, calls=%fused_computation.25 | convolution fusion | flops 6446383104 | bytes 24131584 | tf_op jit(solution)/shard_map/dot_general | solution.py:13
  506.3 14.4 %fusion.218 = (f32[6,128]{1,0:T(8,128)S(1)}, f32[6,128,1024]{2,1,0:T(8,128)S(1)}) fusion(f32[1024]{0:T(1024)S(1)} %copy-done.52, bf16[4096,1024]{1,0:T(8,128)(2,1)} %all-gather.19.cloned.1.call-done, f32[6,128,4096]{2,1,0:T(8,128)} %fusion.22, f32[4096]{0:T(1024)S(1)} %copy-done.49, f32[1024]{0:T(1024)S(1)} %copy-done.53, f32[1024]{0:T(1024)S(1)} %copy-done.46, ...), kind=kOutput, calls=%fused_computation.228 | convolution fusion | flops 6479412224 | bytes 27300864 | tf_op jit(solution)/shard_map/dot_general | solution.py:13
  527.0 22.6 %fusion.222 = (f32[4096]{0:T(1024)S(1)}, bf16[6,128,4096]{2,1,0:T(8,128)(2,1)}) fusion(f32[6,128,4096]{2,1,0:T(8,128)} %fusion.22, f32[4096]{0:T(1024)S(1)} %copy-done.49, bf16[4096,1024]{1,0:T(8,128)(2,1)} %all-gather.19.cloned.1.call-done, f32[6,128]{1,0:T(8,128)S(1)} %negate_multiply_fusion.1, f32[6,128]{1,0:T(8,128)S(1)} %get-tuple-element.40, ...), kind=kOutput, calls=%fused_computation.232 | convolution fusion | flops 6518730752 | bytes 32030720 | tf_op jit(solution)/shard_map/dot_general | solution.py:17
  549.7 13.8 %fusion.211 = (f32[1024]{0:T(1024)S(1)}, f32[6,128]{1,0:T(8,128)S(1)}, f32[6,128,1024]{2,1,0:T(8,128)}) fusion(f32[1024]{0:T(1024)S(1)} %copy-done.46, f32[6,128,1024]{2,1,0:T(8,128)S(1)} %get-tuple-element.47, f32[6,128]{1,0:T(8,128)S(1)} %broadcast_multiply_fusion.1, bf16[1024,4096]{1,0:T(8,128)(2,1)} %all-gather.17.cloned.1.call-done, ...), kind=kOutput, calls=%fused_computation.221 | convolution fusion | flops 6453458944 | bytes 25720832 | tf_op jit(solution)/shard_map/dot_general | solution.py:17
  577.9 7.3 %bitcast_reduce_fusion = (f32[16,64]{1,0:T(8,128)S(1)}, f32[6,16,64,128]{3,2,1,0:T(8,128)}) fusion(bf16[6,128,16,64]{1,3,2,0:T(8,128)(2,1)} %bitcast.214, f32[6,16,128,128]{2,3,1,0:T(8,128)} %get-tuple-element.45, f32[6,16,128]{2,1,0:T(8,128)S(1)} %copy-done.43), kind=kOutput, calls=%fused_computation.64 | convolution fusion | flops 205257728 | bytes 11063296 | tf_op jit(solution)/shard_map/nhqk,nqhd->nkhd/dot_general | solution.py:183
  590.0 6.9 multiply_reduce_fusion.1
  596.9 7.0 %multiply_convert_fusion.2 = bf16[6,16,128,128]{2,3,1,0:T(8,128)(2,1)S(1)} fusion(f32[6,16,128,128]{2,3,1,0:T(8,128)} %get-tuple-element.58, f32[6,16,128]{2,1,0:T(8,128)S(1)} %get-tuple-element.57, f32[6,16,128,128]{2,3,1,0:T(8,128)} %get-tuple-element.45, f32[6,16,128]{2,1,0:T(8,128)S(1)} %copy-done.43), kind=kLoop, calls=%fused_computation.32 | loop fusion | flops 6291456 | bytes 15826944 | tf_op jit(solution)/shard_map/convert_element_type | solution.py:174
  617.9 10.3 %fusion.80 = f32[6,128,1024]{2,1,0:T(8,128)S(1)} fusion(f32[6,128,1024]{1,2,0:T(8,128)S(1)} %bitcast.222, bf16[1024,1024]{1,0:T(8,128)(2,1)S(1)} %copy-done.27), kind=kOutput, calls=%fused_computation.113 | convolution fusion | flops 9663676416 | bytes 8388608 | tf_op jit(solution)/shard_map/dot_general | solution.py:23
  628.2 10.2 %fusion.64 = f32[6,128,1024]{2,1,0:T(8,128)S(1)} fusion(f32[6,128,1024]{1,2,0:T(8,128)S(1)} %bitcast.204, bf16[1024,1024]{1,0:T(8,128)(2,1)S(1)} %copy-done.24), kind=kOutput, calls=%fused_computation.97 | convolution fusion | flops 9663676416 | bytes 8388608 | tf_op jit(solution)/shard_map/dot_general | solution.py:23
  643.4 40.4 %all-reduce = (f32[1024]{0:T(1024)}, f32[1024]{0:T(1024)}, f32[1024]{0:T(1024)}, f32[4096]{0:T(1024)}, f32[1024]{0:T(1024)}, /*index=5*/f32[1024]{0:T(1024)}, f32[1024]{0:T(1024)}) all-reduce(f32[1024]{0:T(1024)S(1)} %reshape.235, f32[1024]{0:T(1024)S(1)} %add.370, ...), channel_id=1, replica_groups=mesh['dp'=8,'seq'=4] {'dp','seq'}, use_global_device_ids=true, to_apply=%region_25.26 | all-reduce | flops 10240 | bytes 81920 | tf_op jit(solution)/shard_map/psum | solution.py:54
  (223 shorter events, 128.7 us)
Async XLA Ops:
  7.2 121.8 %copy-start.35 = (bf16[2,128,1024]{2,1,0:T(8,128)(2,1)S(1)}, bf16[2,128,1024]{2,1,0:T(8,128)(2,1)}, u32[]{:S(2)}) copy-start(bf16[2,128,1024]{2,1,0:T(8,128)(2,1)} %param.22) | copy-start | bytes 1572868
  7.2 63.2 %all-gather.9.cloned.1.call-start = ((), (), s32[]{:S(2)}) async-start(), calls=%async_computation.2 | async-start | bytes 2162688 | tf_op jit(solution)/shard_map/all_gather | solution.py:252
  8.9 120.1 %all-gather.13.cloned.1.call-start = ((), (), s32[]{:S(2)}) async-start(), calls=%async_computation.4 | async-start | bytes 2162688 | tf_op jit(solution)/shard_map/all_gather | solution.py:251
  10.5 177.1 %all-gather.11.cloned.1.call-start = ((), (), s32[]{:S(2)}) async-start(), calls=%async_computation.3 | async-start | bytes 2162688 | tf_op jit(solution)/shard_map/all_gather | solution.py:250
  12.1 233.3 %all-gather.15.cloned.1.call-start = ((), (), s32[]{:S(2)}) async-start(), calls=%async_computation.5 | async-start | bytes 2162688 | tf_op jit(solution)/shard_map/all_gather | solution.py:253
  13.7 255.1 %all-gather.21.cloned.1.call-start = ((), (), s32[]{:S(2)}) async-start(), calls=%async_computation.8 | async-start | bytes 2621440 | tf_op jit(solution)/shard_map/all_gather | solution.py:49
  73.6 58.6 %copy-start.37 = (f32[32,4096]{1,0:T(8,128)S(1)}, f32[32,4096]{1,0:T(8,128)}, u32[]{:S(2)}) copy-start(f32[32,4096]{1,0:T(8,128)} %param.31) | copy-start | bytes 1572868
  73.6 59.4 %copy-start.38 = (f32[128,1024]{1,0:T(8,128)S(1)}, f32[128,1024]{1,0:T(8,128)}, u32[]{:S(2)}) copy-start(f32[128,1024]{1,0:T(8,128)} %param.32) | copy-start | bytes 1572868
  73.6 60.2 %copy-start.54 = (s32[6]{0:T(128)S(1)}, s32[6]{0:T(128)}, u32[]{:S(2)}) copy-start(s32[6]{0:T(128)} %param.25) | copy-start | bytes 76
  73.7 60.3 %copy-start.48 = (s32[2]{0:T(128)S(1)}, s32[2]{0:T(128)}, u32[]{:S(2)}) copy-start(s32[2]{0:T(128)} %param.26) | copy-start | bytes 28
  73.7 113.9 %copy-start.51 = (f32[1024]{0:T(1024)S(1)}, f32[1024]{0:T(1024)}, u32[]{:S(2)}) copy-start(f32[1024]{0:T(1024)} %param.33) | copy-start | bytes 12292
  73.7 219.2 %all-gather.23.cloned.1.call-start = ((), (), s32[]{:S(2)}) async-start(), calls=%async_computation.9 | async-start | bytes 2621440 | tf_op jit(solution)/shard_map/all_gather | solution.py:48
  132.1 240.7 %all-gather.17.cloned.1.call-start = ((), (), s32[]{:S(2)}) async-start(), calls=%async_computation.6 | async-start | bytes 8650752 | tf_op jit(solution)/shard_map/all_gather | solution.py:254
  132.9 57.9 %copy-start.23 = (bf16[6,128,1024]{2,1,0:T(8,128)(2,1)S(1)}, bf16[6,128,1024]{2,1,0:T(8,128)(2,1)}, u32[]{:S(2)}) copy-start(bf16[6,128,1024]{2,1,0:T(8,128)(2,1)} %param.21) | copy-start | bytes 4718596
  132.9 57.9 %copy-start.50 = (f32[1024]{0:T(1024)S(1)}, f32[1024]{0:T(1024)}, u32[]{:S(2)}) copy-start(f32[1024]{0:T(1024)} %param.34) | copy-start | bytes 12292
  133.0 318.4 %all-gather.19.cloned.1.call-start = ((), (), s32[]{:S(2)}) async-start(), calls=%async_computation.7 | async-start | bytes 8650752 | tf_op jit(solution)/shard_map/all_gather | solution.py:255
  133.8 508.4 %reduce-scatter.5.cloned.1.call-start = ((), (), s32[]{:S(2)}) async-start(), calls=%async_computation.11 | async-start | bytes 2621440 | tf_op jit(solution)/shard_map/reduce_scatter | solution.py:68
  310.8 62.0 %copy-start.46 = (f32[1024]{0:T(1024)S(1)}, f32[1024]{0:T(1024)}, u32[]{:S(2)}) copy-start(f32[1024]{0:T(1024)} %param.38) | copy-start | bytes 12292
  310.8 62.0 %copy-start.49 = (f32[4096]{0:T(1024)S(1)}, f32[4096]{0:T(1024)}, u32[]{:S(2)}) copy-start(f32[4096]{0:T(1024)} %param.36) | copy-start | bytes 49156
  310.8 62.0 %copy-start.53 = (f32[1024]{0:T(1024)S(1)}, f32[1024]{0:T(1024)}, u32[]{:S(2)}) copy-start(f32[1024]{0:T(1024)} %param.39) | copy-start | bytes 12292
  312.9 138.5 %copy-start.52 = (f32[1024]{0:T(1024)S(1)}, f32[1024]{0:T(1024)}, u32[]{:S(2)}) copy-start(f32[1024]{0:T(1024)} %param.37) | copy-start | bytes 12292
  380.9 78.3 %copy-start.40 = (f32[1024]{0:T(1024)S(1)}, f32[1024]{0:T(1024)}, u32[]{:S(2)}) copy-start(f32[1024]{0:T(1024)} %param.40) | copy-start | bytes 12292
  493.2 190.5 %reduce-scatter.3.cloned.1.call-start = ((), (), s32[]{:S(2)}) async-start(), calls=%async_computation.10 | async-start | bytes 2621440 | tf_op jit(solution)/shard_map/reduce_scatter | solution.py:65
  527.0 36.4 %copy-start = (bf16[2,16,128,512]{3,2,1,0:T(8,128)(2,1)}, bf16[2,16,128,512]{3,2,1,0:T(8,128)(2,1)S(1)}, u32[]{:S(2)}) copy-start(bf16[2,16,128,512]{3,2,1,0:T(8,128)(2,1)S(1)} %multiply_convert_fusion.1) | copy-start | bytes 12582916
  (47 other events, 296.8 us)
Sparse Core Ops, SparseCore 0:
  11.4 58.9 all-gather.8
  73.9 55.0 all-gather.12
  132.4 55.0 all-gather.10
  190.3 55.0 all-gather.14
  247.4 21.4 all-gather.20
  270.2 22.5 all-gather.22
  295.7 77.0 all-gather.16
  375.7 75.6 all-gather.18
  493.3 29.7 reduce-scatter.4
  597.0 29.7 reduce-scatter.2
where the time goes:
time: 704 us; the launch traced here: 695 us
  waiting for transfers between devices  360 us (51%)
  matrix products  211 us (30%)
  blocking collectives  40.4 us (6%)
  local copies, waits for them, and re-layouts  34.1 us (5%)
  other arithmetic  33 us (5%)
  between operations  15.4 us (2%)
    all_gather x1, waiting for transfers between devices, on_device(): lax.all_gather(downward_low, ('dp', 'seq'), axis=0, tiled=True)  70.5 us
    dot_general x12, matrix products, forward_product(): return jnp.dot(left, right, preferred_element_type=jnp.float32)  70.3 us
    all_gather x1, waiting for transfers between devices, on_device(): lax.all_gather(upward_low, ('dp', 'seq'), axis=0, tiled=True)  59.9 us
    all_gather x1, waiting for transfers between devices, on_device(): lax.all_gather(value_low, ('dp', 'seq'), axis=0, tiled=True)  56.7 us
    dot_general x8, matrix products, backward_product(): lax.dot_general(left, right, (((left.ndim - 1,), (1,)), ((), ())), prefer...  55.5 us
    all_gather x1, waiting for transfers between devices, on_device(): lax.all_gather(key_low, ('dp', 'seq'), axis=0, tiled=True)  55.3 us
    all_gather x1, waiting for transfers between devices, on_device(): lax.all_gather(query_low, ('dp', 'seq'), axis=0, tiled=True)  53.6 us
    psum x1, blocking collectives, settle_each(): return lax.psum(value, ('dp', 'seq'))  40.4 us
  transfers between devices with their start and end apart: 10, of which 8 were waited for; matrix products, arithmetic and copies ran while one was open for 32% of the time, Pallas kernels for 0%

commit v1 on v0

--- a/solution.py
+++ b/solution.py
@@ -51,7 +51,7 @@
 
 
 def settle_each(value):
-    return lax.psum(value, ("dp", "seq"))
+    return jnp.sum(lax.all_gather(value, ("dp", "seq")), axis=0)
 
 
 def finish_local(key_terms, value_terms, key_exact, value_exact, settle):

time: 704 us -> 1200 us (1.70)
  blocking collectives: 40.4 us -> 535 us
    all_gather x0 -> x14, blocking collectives: none -> 535 us  [settle_each(): return jnp.sum(lax.all_gather(value, ('dp', 'seq')), axis=0)]
    psum x1 -> x0, blocking collectives: 40.4 us -> none  [settle_each(): return lax.psum(value, ('dp', 'seq'))]
  transfers between devices with their start and end apart: 10 -> 10, of which waited for: 8 -> 8; matrix products, arithmetic and copies ran while one was open for 32% -> 19% of each run, Pallas kernels for 0% -> 0%
where the time goes in v1:
time: 1200 us; the launch traced here: 1190 us
  blocking collectives  535 us (45%)
  waiting for transfers between devices  361 us (30%)
  matrix products  210 us (18%)
  other arithmetic  40.3 us (3%)
  local copies, waits for them, and re-layouts  32.9 us (3%)
  between operations  15.5 us (1%)
    all_gather x14, blocking collectives, settle_each(): return jnp.sum(lax.all_gather(value, ('dp', 'seq')), axis=0)  535 us
    all_gather x1, waiting for transfers between devices, on_device(): lax.all_gather(downward_low, ('dp', 'seq'), axis=0, tiled=True)  70.4 us
    dot_general x12, matrix products, forward_product(): return jnp.dot(left, right, preferred_element_type=jnp.float32)  68.6 us
    dot_general x8, matrix products, backward_product(): lax.dot_general(left, right, (((left.ndim - 1,), (1,)), ((), ())), prefer...  60.7 us
    all_gather x1, waiting for transfers between devices, on_device(): lax.all_gather(upward_low, ('dp', 'seq'), axis=0, tiled=True)  60 us
    all_gather x1, waiting for transfers between devices, on_device(): lax.all_gather(value_low, ('dp', 'seq'), axis=0, tiled=True)  56.7 us
    all_gather x1, waiting for transfers between devices, on_device(): lax.all_gather(key_low, ('dp', 'seq'), axis=0, tiled=True)  55.3 us
    all_gather x1, waiting for transfers between devices, on_device(): lax.all_gather(query_low, ('dp', 'seq'), axis=0, tiled=True)  53.5 us
  transfers between devices with their start and end apart: 10, of which 8 were waited for; matrix products, arithmetic and copies ran while one was open for 19% of the time, Pallas kernels for 0%

profile of v1, /device:TPU:0, one launch (start us, length us, event | category | flops | bytes accessed | tf_op | source)
XLA Modules:
  0.0 1194.9 jit_solution(9154295597155534078)
XLA Ops:
  13.8 56.7 %all-gather.23.cloned.1.call-done = bf16[1024,1024]{1,0:T(8,128)(2,1)} async-done(((bf16[32,1024]{1,0:T(8,128)(2,1)}), bf16[1024,1024]{1,0:T(8,128)(2,1)}) %all-gather.23.cloned.1.call-update) | async-done | bytes 2097168 | tf_op jit(solution)/shard_map/all_gather | solution.py:252
  73.7 55.3 %all-gather.27.cloned.1.call-done = bf16[1024,1024]{1,0:T(8,128)(2,1)} async-done(((bf16[32,1024]{1,0:T(8,128)(2,1)}), bf16[1024,1024]{1,0:T(8,128)(2,1)}) %all-gather.27.cloned.1.call-update) | async-done | bytes 2097168 | tf_op jit(solution)/shard_map/all_gather | solution.py:251
  134.0 53.5 %all-gather.25.cloned.1.call-done = bf16[1024,1024]{1,0:T(8,128)(2,1)} async-done(((bf16[32,1024]{1,0:T(8,128)(2,1)}), bf16[1024,1024]{1,0:T(8,128)(2,1)}) %all-gather.25.cloned.1.call-update) | async-done | bytes 2097168 | tf_op jit(solution)/shard_map/all_gather | solution.py:250
  219.2 26.2 %all-gather.29.cloned.1.call-done = bf16[1024,1024]{1,0:T(8,128)(2,1)} async-done(((bf16[32,1024]{1,0:T(8,128)(2,1)}), bf16[1024,1024]{1,0:T(8,128)(2,1)}) %all-gather.29.cloned.1.call-update) | async-done | bytes 2097168 | tf_op jit(solution)/shard_map/all_gather | solution.py:253
  250.4 18.4 %all-gather.35.cloned.1.call-done = bf16[2,512,1024]{2,1,0:T(8,128)(2,1)} async-done(((bf16[2,128,1024]{2,1,0:T(8,128)(2,1)}), bf16[2,512,1024]{2,1,0:T(8,128)(2,1)}) %all-gather.35.cloned.1.call-update) | async-done | bytes 2097168 | tf_op jit(solution)/shard_map/all_gather | solution.py:49
  272.8 20.1 %all-gather.37.cloned.1.call-done = bf16[2,512,1024]{2,1,0:T(8,128)(2,1)} async-done(((bf16[2,128,1024]{2,1,0:T(8,128)(2,1)}), bf16[2,512,1024]{2,1,0:T(8,128)(2,1)}) %all-gather.37.cloned.1.call-update) | async-done | bytes 2097168 | tf_op jit(solution)/shard_map/all_gather | solution.py:48
  312.8 60.0 %all-gather.31.cloned.1.call-done = bf16[1024,4096]{1,0:T(8,128)(2,1)} async-done(((bf16[32,4096]{1,0:T(8,128)(2,1)}), bf16[1024,4096]{1,0:T(8,128)(2,1)}) %all-gather.31.cloned.1.call-update) | async-done | bytes 8388624 | tf_op jit(solution)/shard_map/all_gather | solution.py:254
  380.9 70.4 %all-gather.33.cloned.1.call-done = bf16[4096,1024]{1,0:T(8,128)(2,1)} async-done(((bf16[128,1024]{1,0:T(8,128)(2,1)}), bf16[4096,1024]{1,0:T(8,128)(2,1)}) %all-gather.33.cloned.1.call-update) | async-done | bytes 8388624 | tf_op jit(solution)/shard_map/all_gather | solution.py:255
  494.7 43.3 %all-gather.4 = f32[131072]{0:T(1024)} all-gather(f32[4096]{0:T(1024)S(1)} %get-tuple-element.60), channel_id=6, replica_groups=mesh['dp'=8,'seq'=4] {'dp','seq'}, dimensions={0}, use_global_device_ids=true | all-gather | bytes 540672 | tf_op jit(solution)/shard_map/all_gather | solution.py:54
  539.9 37.0 %all-gather.2 = f32[32768]{0:T(1024)S(1)} all-gather(f32[1024]{0:T(1024)S(1)} %add_reduce_fusion.2), channel_id=4, replica_groups=mesh['dp'=8,'seq'=4] {'dp','seq'}, dimensions={0}, use_global_device_ids=true | all-gather | bytes 135168 | tf_op jit(solution)/shard_map/all_gather | solution.py:54
  590.4 16.3 %fusion.218 = (f32[6,128]{1,0:T(8,128)S(1)}, f32[6,128,1024]{2,1,0:T(8,128)S(1)}) fusion(f32[1024]{0:T(1024)S(1)} %copy-done.58, bf16[4096,1024]{1,0:T(8,128)(2,1)} %all-gather.33.cloned.1.call-done, f32[6,128,4096]{2,1,0:T(8,128)S(1)} %fusion.22, f32[4096]{0:T(1024)S(1)} %copy-done.55, f32[1024]{0:T(1024)S(1)} %copy-done.59, f32[1024]{0:T(1024)S(1)} %copy-done.43, ...), kind=kOutput, calls=%fused_computation.228 | convolution fusion | flops 6479412224 | bytes 27300864 | tf_op jit(solution)/shard_map/dot_general | solution.py:13
  608.8 21.7 %fusion.222 = (f32[4096]{0:T(1024)}, bf16[6,128,4096]{2,1,0:T(8,128)(2,1)}) fusion(f32[6,128,4096]{2,1,0:T(8,128)} %copy-done.63, f32[4096]{0:T(1024)S(1)} %copy-done.55, bf16[4096,1024]{1,0:T(8,128)(2,1)} %all-gather.33.cloned.1.call-done, f32[6,128]{1,0:T(8,128)S(1)} %negate_multiply_fusion.1, f32[6,128]{1,0:T(8,128)S(1)} %get-tuple-element.33, ...), kind=kOutput, calls=%fused_computation.232 | convolution fusion | flops 6518730752 | bytes 32030720 | tf_op jit(solution)/shard_map/dot_general | solution.py:17
  649.4 38.3 %all-gather.10 = f32[32768]{0:T(1024)S(1)} all-gather(f32[1024]{0:T(1024)S(1)} %get-tuple-element.21), channel_id=12, replica_groups=mesh['dp'=8,'seq'=4] {'dp','seq'}, dimensions={0}, use_global_device_ids=true | all-gather | bytes 135168 | tf_op jit(solution)/shard_map/all_gather | solution.py:54
  690.3 37.4 %all-gather.8 = f32[32768]{0:T(1024)S(1)} all-gather(f32[1024]{0:T(1024)} %get-tuple-element.19), channel_id=10, replica_groups=mesh['dp'=8,'seq'=4] {'dp','seq'}, dimensions={0}, use_global_device_ids=true | all-gather | bytes 135168 | tf_op jit(solution)/shard_map/all_gather | solution.py:54
  727.7 38.5 %all-gather.6 = f32[32768]{0:T(1024)S(1)} all-gather(f32[1024]{0:T(1024)} %get-tuple-element.22), channel_id=8, replica_groups=mesh['dp'=8,'seq'=4] {'dp','seq'}, dimensions={0}, use_global_device_ids=true | all-gather | bytes 135168 | tf_op jit(solution)/shard_map/all_gather | solution.py:54
  771.1 37.4 %all-gather.12 = f32[32,1,1024]{2,1,0:T(1,128)S(1)} all-gather(f32[1,1,1024]{2,1,0:T(1,128)S(1)} %reshape.251), channel_id=1, replica_groups=mesh['dp'=8,'seq'=4] {'dp','seq'}, dimensions={0}, use_global_device_ids=true | all-gather | bytes 135168 | tf_op jit(solution)/shard_map/all_gather | solution.py:54
  818.1 38.2 %all-gather.1 = f32[32768]{0:T(1024)S(1)} all-gather(f32[1024]{0:T(1024)S(1)} %add_reduce_fusion), channel_id=3, replica_groups=mesh['dp'=8,'seq'=4] {'dp','seq'}, dimensions={0}, use_global_device_ids=true | all-gather | bytes 135168 | tf_op jit(solution)/shard_map/all_gather | solution.py:54
  856.4 37.1 %all-gather.7 = f32[32768]{0:T(1024)S(1)} all-gather(f32[1024]{0:T(1024)S(1)} %copy-done.53), channel_id=9, replica_groups=mesh['dp'=8,'seq'=4] {'dp','seq'}, dimensions={0}, use_global_device_ids=true | all-gather | bytes 135168 | tf_op jit(solution)/shard_map/all_gather | solution.py:54
  897.2 38.3 %all-gather.9 = f32[32768]{0:T(1024)S(1)} all-gather(f32[1024]{0:T(1024)S(1)} %get-tuple-element.15), channel_id=11, replica_groups=mesh['dp'=8,'seq'=4] {'dp','seq'}, dimensions={0}, use_global_device_ids=true | all-gather | bytes 135168 | tf_op jit(solution)/shard_map/all_gather | solution.py:54
  935.6 37.1 %all-gather.5 = f32[32768]{0:T(1024)S(1)} all-gather(f32[1024]{0:T(1024)S(1)} %get-tuple-element.16), channel_id=7, replica_groups=mesh['dp'=8,'seq'=4] {'dp','seq'}, dimensions={0}, use_global_device_ids=true | all-gather | bytes 135168 | tf_op jit(solution)/shard_map/all_gather | solution.py:54
  972.8 39.3 %all-gather.3 = f32[131072]{0:T(1024)S(1)} all-gather(f32[4096]{0:T(1024)S(1)} %copy-done.49), channel_id=5, replica_groups=mesh['dp'=8,'seq'=4] {'dp','seq'}, dimensions={0}, use_global_device_ids=true | all-gather | bytes 540672 | tf_op jit(solution)/shard_map/all_gather | solution.py:54
  1019.1 37.0 %all-gather.13 = f32[32,1,1024]{2,1,0:T(1,128)S(1)} all-gather(f32[1,1,1024]{2,1,0:T(1,128)S(1)} %reshape.253), channel_id=1, replica_groups=mesh['dp'=8,'seq'=4] {'dp','seq'}, dimensions={0}, use_global_device_ids=true | all-gather | bytes 135168 | tf_op jit(solution)/shard_map/all_gather | solution.py:54
  1072.6 38.5 %all-gather.11 = f32[32,1,1024]{2,1,0:T(1,128)S(1)} all-gather(f32[1,1,1024]{2,1,0:T(1,128)S(1)} %reshape.249), channel_id=1, replica_groups=mesh['dp'=8,'seq'=4] {'dp','seq'}, dimensions={0}, use_global_device_ids=true | all-gather | bytes 135168 | tf_op jit(solution)/shard_map/all_gather | solution.py:54
  1146.1 37.3 %all-gather = f32[32768]{0:T(1024)S(1)} all-gather(f32[1024]{0:T(1024)S(1)} %convert_reduce_fusion.2), channel_id=2, replica_groups=mesh['dp'=8,'seq'=4] {'dp','seq'}, dimensions={0}, use_global_device_ids=true | all-gather | bytes 135168 | tf_op jit(solution)/shard_map/all_gather | solution.py:54
  (276 shorter events, 245.8 us)
Async XLA Ops:
  7.2 121.8 %copy-start.31 = (bf16[2,128,1024]{2,1,0:T(8,128)(2,1)S(1)}, bf16[2,128,1024]{2,1,0:T(8,128)(2,1)}, u32[]{:S(2)}) copy-start(bf16[2,128,1024]{2,1,0:T(8,128)(2,1)} %param.22) | copy-start | bytes 1572868
  7.2 63.2 %all-gather.23.cloned.1.call-start = ((), (), s32[]{:S(2)}) async-start(), calls=%async_computation.2 | async-start | bytes 2162688 | tf_op jit(solution)/shard_map/all_gather | solution.py:252
  8.8 120.1 %all-gather.27.cloned.1.call-start = ((), (), s32[]{:S(2)}) async-start(), calls=%async_computation.4 | async-start | bytes 2162688 | tf_op jit(solution)/shard_map/all_gather | solution.py:251
  10.5 177.1 %all-gather.25.cloned.1.call-start = ((), (), s32[]{:S(2)}) async-start(), calls=%async_computation.3 | async-start | bytes 2162688 | tf_op jit(solution)/shard_map/all_gather | solution.py:250
  12.1 233.3 %all-gather.29.cloned.1.call-start = ((), (), s32[]{:S(2)}) async-start(), calls=%async_computation.5 | async-start | bytes 2162688 | tf_op jit(solution)/shard_map/all_gather | solution.py:253
  13.7 255.1 %all-gather.35.cloned.1.call-start = ((), (), s32[]{:S(2)}) async-start(), calls=%async_computation.8 | async-start | bytes 2621440 | tf_op jit(solution)/shard_map/all_gather | solution.py:49
  73.7 113.9 %copy-start.57 = (f32[1024]{0:T(1024)S(1)}, f32[1024]{0:T(1024)}, u32[]{:S(2)}) copy-start(f32[1024]{0:T(1024)} %param.33) | copy-start | bytes 12292
  73.7 219.2 %all-gather.37.cloned.1.call-start = ((), (), s32[]{:S(2)}) async-start(), calls=%async_computation.9 | async-start | bytes 2621440 | tf_op jit(solution)/shard_map/all_gather | solution.py:48
  132.1 240.7 %all-gather.31.cloned.1.call-start = ((), (), s32[]{:S(2)}) async-start(), calls=%async_computation.6 | async-start | bytes 8650752 | tf_op jit(solution)/shard_map/all_gather | solution.py:254
  133.0 318.4 %all-gather.33.cloned.1.call-start = ((), (), s32[]{:S(2)}) async-start(), calls=%async_computation.7 | async-start | bytes 8650752 | tf_op jit(solution)/shard_map/all_gather | solution.py:255
  133.8 1011.1 %reduce-scatter.5.cloned.1.call-start = ((), (), s32[]{:S(2)}) async-start(), calls=%async_computation.11 | async-start | bytes 2621440 | tf_op jit(solution)/shard_map/reduce_scatter | solution.py:68
  310.6 62.2 %copy-start.43 = (f32[1024]{0:T(1024)S(1)}, f32[1024]{0:T(1024)}, u32[]{:S(2)}) copy-start(f32[1024]{0:T(1024)} %param.38) | copy-start | bytes 12292
  310.6 62.2 %copy-start.55 = (f32[4096]{0:T(1024)S(1)}, f32[4096]{0:T(1024)}, u32[]{:S(2)}) copy-start(f32[4096]{0:T(1024)} %param.36) | copy-start | bytes 49156
  312.8 138.6 %copy-start.58 = (f32[1024]{0:T(1024)S(1)}, f32[1024]{0:T(1024)}, u32[]{:S(2)}) copy-start(f32[1024]{0:T(1024)} %param.37) | copy-start | bytes 12292
  380.9 78.3 %copy-start.36 = (f32[1024]{0:T(1024)S(1)}, f32[1024]{0:T(1024)}, u32[]{:S(2)}) copy-start(f32[1024]{0:T(1024)} %param.40) | copy-start | bytes 12292
  581.0 603.0 %reduce-scatter.3.cloned.1.call-start = ((), (), s32[]{:S(2)}) async-start(), calls=%async_computation.10 | async-start | bytes 2621440 | tf_op jit(solution)/shard_map/reduce_scatter | solution.py:65
  689.6 119.0 %copy-start.3 = (f32[6,128,1024]{2,1,0:T(8,128)S(1)}, f32[6,128,1024]{2,1,0:T(8,128)}, u32[]{:S(2)}) copy-start(f32[6,128,1024]{2,1,0:T(8,128)} %get-tuple-element.26) | copy-start | bytes 9437188
  690.2 118.4 %copy-start.48 = (f32[6,128]{1,0:T(8,128)S(1)}, f32[6,128]{1,0:T(8,128)}, u32[]{:S(2)}) copy-start(f32[6,128]{1,0:T(8,128)} %get-tuple-element.25) | copy-start | bytes 9220
  813.2 80.4 %copy-start.1 = (f32[6,128,1024]{2,1,0:T(8,128)S(1)}, f32[6,128,1024]{2,1,0:T(8,128)}, u32[]{:S(2)}) copy-start(f32[6,128,1024]{2,1,0:T(8,128)} %copy-done) | copy-start | bytes 9437188
  813.2 80.4 %copy-start.45 = (f32[1024]{0:T(1024)S(1)}, f32[1024]{0:T(1024)}, u32[]{:S(2)}) copy-start(f32[1024]{0:T(1024)} %param.41) | copy-start | bytes 12292
  813.2 80.4 %copy-start.47 = (f32[6,128]{1,0:T(8,128)S(1)}, f32[6,128]{1,0:T(8,128)}, u32[]{:S(2)}) copy-start(f32[6,128]{1,0:T(8,128)} %copy-done.46) | copy-start | bytes 9220
  893.6 79.1 %copy-start.49 = (f32[4096]{0:T(1024)S(1)}, f32[4096]{0:T(1024)}, u32[]{:S(2)}) copy-start(f32[4096]{0:T(1024)} %get-tuple-element.58) | copy-start | bytes 49156
  897.2 115.0 %copy-start.29 = (bf16[6,128,1024]{1,2,0:T(8,128)(2,1)S(1)}, bf16[6,128,1024]{1,2,0:T(8,128)(2,1)}, u32[]{:S(2)}) copy-start(bf16[6,128,1024]{1,2,0:T(8,128)(2,1)} %copy.109) | copy-start | bytes 4718596
  897.2 115.0 %copy-start.40 = (f32[6,16,128]{2,1,0:T(8,128)S(1)}, f32[6,16,128]{2,1,0:T(8,128)}, u32[]{:S(2)}) copy-start(f32[6,16,128]{2,1,0:T(8,128)} %copy-done.39) | copy-start | bytes 147460
  (54 other events, 1170.1 us)
Sparse Core Ops, SparseCore 0:
  11.4 58.9 all-gather.22
  73.9 55.0 all-gather.26
  132.4 55.0 all-gather.24
  190.3 55.0 all-gather.28
  247.4 21.4 all-gather.34
  270.2 22.5 all-gather.36
  295.7 77.0 all-gather.30
  375.7 75.6 all-gather.32
  581.1 28.6 reduce-scatter.4
  1063.2 29.0 reduce-scatter.2
